TPU v7x, 32 devices: a whole 2x2x4 slice. The times are simulated.
32 devices in a mesh: gx: 4 (over z), gy: 8 (over y, x, core).
Axes of the slice: x: 2, y: 2, z: 4, core: 2. Of those that a mesh axis runs over, the one named last changes fastest.
Arguments:
- factor: bfloat16 [256, 256, 768], P(('gx', 'gy')), may hold values from -0.21875 to 0.21875
- right_sides: bfloat16 [65536, 128], P(('gx', 'gy')), may hold values from -6 to 6
- send_rows: int32 [32, 32, 48], P(('gx', 'gy')), may hold values from 0 to 2047, as said below
- neighbour_slot: int32 [256, 512], P(('gx', 'gy')), may hold values from 0 to 1536, as said below
Outputs:
- half_product: bfloat16 [65536, 128], P(('gx', 'gy'))
- full_product: bfloat16 [65536, 128], P(('gx', 'gy'))
Inputs may be any that keep to these rules, and one draw needn't show every extreme that they name: `send_rows`: devices follow an ordering drawn with the tables, and device d receives only from owners e that precede it. For each owner e and receiver d the first c[d, e] places hold distinct rows and the rest hold 0, where c[d, e] is at most 48; every device but the first in the ordering receives 48 rows from the owner just before it, and the c[d, e] of one receiver sum to at most 1024. `neighbour_slot`: an entry is either a live place (p below c[d, e]) or 1536, which marks padding; the live entries of one block are distinct, and every live place of a device is named by exactly 4 of that device's blocks.
All inputs are finite; a program needn't handle non-finite values.
Results may differ from a plain program's by a relative error of at most 0.0047.
Values may be sent and summed in bfloat16 or wider, within the bound.
A program may use at most 64 MiB of HBM per device.

v0:
```python
import functools

import jax
import jax.numpy as jnp
from jax import lax
from jax.experimental import pallas as pl
from jax.experimental.pallas import tpu as pltpu
from jax.sharding import PartitionSpec as P

MESH = pl.DeviceIdType.MESH
NT = (((1,), (1,)), ((), ()))
TN = (((0,), (0,)), ((), ()))


def one_hot(mask):
    return jnp.where(mask, 1.0, 0.0).astype(jnp.bfloat16)


def kernel(
    outer, inner, tile,
    factor_ref, vector_ref, table_ref, slots_ref, half, full,
    factor, vector, spread, spread_t, picker, packed, received, sums, returned, rows_ref, total,
    load_sem, go_sem, come_sem, back_go_sem, back_come_sem,
):
    blocks, width, _ = factor.shape
    rows_here, columns = vector.shape
    senders, capacity, _ = packed.shape
    places = senders * capacity
    span = inner * capacity
    gx, gy = lax.axis_index("gx"), lax.axis_index("gy")
    me = gx * inner + gy

    def peer(k):
        other = lax.rem(me + k, senders)
        return (other // inner, lax.rem(other, inner))

    barrier = pltpu.get_barrier_semaphore()

    def greet(k, carry):
        pl.semaphore_signal(barrier, inc=1, device_id=peer(k), device_id_type=MESH)
        return carry

    lax.fori_loop(1, senders, greet, 0)
    load_vector = pltpu.make_async_copy(vector_ref, vector, load_sem.at[0])
    load_factor = pltpu.make_async_copy(factor_ref, factor, load_sem.at[1])
    load_vector.start()
    load_factor.start()

    far_order = [z for z in (outer // 2, *range(1, outer)) if z]
    order = list(dict.fromkeys(far_order)) + [0]

    received[me] = jnp.zeros((capacity, columns), jnp.bfloat16)
    returned[me] = jnp.zeros((capacity, columns), jnp.bfloat16)

    def plane(z):
        return lax.rem(gx + z, outer)

    def group_places(g):
        return pl.ds(pl.multiple_of(g * span, 128), span)

    def group(ref, g):
        return ref[pl.ds(g * inner, inner)].reshape(span, columns)

    def copy_of(source, target, send_sem, recv_sem, z, y):
        to_x, to_y = plane(z), lax.rem(gy + y, inner)
        other = to_x * inner + to_y
        return pltpu.make_async_remote_copy(
            src_ref=source.at[other],
            dst_ref=target.at[me],
            send_sem=send_sem.at[other],
            recv_sem=recv_sem.at[me],
            device_id=(to_x, to_y),
            device_id_type=MESH,
        )

    def send_group(source, target, send_sem, recv_sem, z):
        def step(y, carry):
            copy_of(source, target, send_sem, recv_sem, z, y).start()
            return carry

        lax.fori_loop(0 if z else 1, inner, step, 0)

    def await_group(source, target, send_sem, recv_sem, z):
        from_x = plane(z)

        def step(y, carry):
            other = from_x * inner + lax.rem(gy + y, inner)
            pltpu.make_async_remote_copy(
                src_ref=source.at[me],
                dst_ref=target.at[other],
                send_sem=send_sem.at[me],
                recv_sem=recv_sem.at[other],
                device_id=(from_x, lax.rem(gy + y, inner)),
                device_id_type=MESH,
            ).wait_recv()
            return carry

        lax.fori_loop(0 if z else 1, inner, step, 0)

    def await_sends(source, target, send_sem, recv_sem):
        for z in order:
            def step(y, carry, z=z):
                copy_of(source, target, send_sem, recv_sem, z, y).wait_send()
                return carry

            lax.fori_loop(0 if z else 1, inner, step, 0)

    outward = (packed, received, go_sem, come_sem)
    inward = (sums, returned, back_go_sem, back_come_sem)

    rows_ref[...] = jnp.concatenate([table_ref[0, e : e + 1, :] for e in range(senders)], axis=1)
    load_vector.wait()

    def pack(g, carry):
        ids = jnp.broadcast_to(rows_ref[0:1, group_places(g)], (128, span)).T
        ids = jnp.concatenate([ids] * (tile // 128), axis=1)
        lane = lax.broadcasted_iota(jnp.int32, (span, tile), 1)
        rows = jnp.zeros((span, columns), jnp.float32)
        for c in range(rows_here // tile):
            rows = rows + jnp.dot(
                one_hot(ids == lane + c * tile),
                vector[c * tile : (c + 1) * tile, :],
                preferred_element_type=jnp.float32,
            )
        packed[pl.ds(g * inner, inner)] = rows.astype(jnp.bfloat16).reshape(inner, capacity, columns)
        return carry

    lax.fori_loop(0, outer, pack, 0)
    load_factor.wait()

    def spread_block(b, carry):
        here = pl.ds(pl.multiple_of(b * width, width), width)
        far = factor[b, :, width:]
        ids = slots_ref[pl.ds(b, 1), :]
        for c in range(places // tile):
            place = lax.broadcasted_iota(jnp.int32, (tile, far.shape[1]), 0) + c * tile
            pick = one_hot(ids == place)
            there = slice(c * tile, (c + 1) * tile)
            spread_t[there, here] = lax.dot_general(
                pick, far, NT, preferred_element_type=jnp.float32
            ).astype(jnp.bfloat16)
            spread[here, there] = lax.dot_general(
                far, pick, NT, preferred_element_type=jnp.float32
            ).astype(jnp.bfloat16)
        total[here, :] = jnp.dot(
            factor[b, :, :width], vector[here, :], preferred_element_type=jnp.float32
        )
        return carry

    pl.semaphore_wait(barrier, senders - 1)
    for z in order:
        send_group(*outward, z)
    lax.fori_loop(0, blocks, spread_block, 0)

    wait_order = [0] + [(outer - z) % outer for z in order if z]
    slab = rows_here // 2
    for n, z in enumerate(wait_order):
        g = plane(z)
        await_group(*outward, z)
        rows = group(received, g)
        for h in range(2):
            part = pl.ds(h * slab, slab)
            value = total[part, :] + jnp.dot(
                spread[part, group_places(g)], rows, preferred_element_type=jnp.float32
            )
            if n < outer - 1:
                total[part, :] = value
            else:
                half[part, :] = value.astype(jnp.bfloat16)

    for z in order:
        g = plane(z)
        value = jnp.dot(
            spread_t[pl.ds(pl.multiple_of(g * span, 128), span), :], half[...],
            preferred_element_type=jnp.float32,
        )
        sums[pl.ds(g * inner, inner)] = value.astype(jnp.bfloat16).reshape(inner, capacity, columns)
        send_group(*inward, z)

    def own_block(b, carry):
        here = pl.ds(pl.multiple_of(b * width, width), width)
        total[here, :] = lax.dot_general(
            factor[b, :, :width], half[here, :], TN, preferred_element_type=jnp.float32
        )
        place = lax.broadcasted_iota(jnp.int32, (width, places), 0) + b * width
        picker[here, :] = one_hot(rows_ref[0:1, :] == place)
        return carry

    lax.fori_loop(0, blocks, own_block, 0)
    await_sends(*outward)

    for n, z in enumerate(wait_order):
        g = plane(z)
        await_group(*inward, z)
        rows = group(returned, g)
        for h in range(2):
            part = pl.ds(h * slab, slab)
            value = total[part, :] + jnp.dot(
                picker[part, group_places(g)], rows, preferred_element_type=jnp.float32
            )
            if n < outer - 1:
                total[part, :] = value
            else:
                full[part, :] = value.astype(jnp.bfloat16)
    await_sends(*inward)


def write_out(half_ref, full_ref, half_out, full_out, sems):
    copies = [
        pltpu.make_async_copy(half_ref, half_out, sems.at[0]),
        pltpu.make_async_copy(full_ref, full_out, sems.at[1]),
    ]
    for copy in copies:
        copy.start()
    for copy in copies:
        copy.wait()


def fused(factor, right_sides, send_rows, neighbour_slot, tile):
    blocks, width, _ = factor.shape
    rows_here, columns = right_sides.shape
    _, senders, capacity = send_rows.shape
    places = senders * capacity
    outer, inner = lax.axis_size("gx"), lax.axis_size("gy")
    kept = jnp.bfloat16
    out = pltpu.VMEM((rows_here, columns), kept)
    moved = pltpu.VMEM((senders, capacity, columns), kept)
    flags = pltpu.SemaphoreType.DMA((senders,))
    half, full = pl.pallas_call(
        functools.partial(kernel, outer, inner, tile),
        out_shape=(out, out),
        in_specs=[pl.BlockSpec(memory_space=pl.ANY)] * 2
        + [pl.BlockSpec(memory_space=pltpu.VMEM)] * 2,
        out_specs=(pl.BlockSpec(memory_space=pltpu.VMEM),) * 2,
        scratch_shapes=[
            pltpu.VMEM(factor.shape, kept),
            pltpu.VMEM((rows_here, columns), kept),
            pltpu.VMEM((rows_here, places), kept),
            pltpu.VMEM((places, rows_here), kept),
            pltpu.VMEM((rows_here, places), kept),
            moved, moved, moved, moved,
            pltpu.VMEM((1, places), jnp.int32),
            pltpu.VMEM((rows_here, columns), jnp.float32),
            pltpu.SemaphoreType.DMA((2,)),
            flags, flags, flags, flags,
        ],
        compiler_params=pltpu.CompilerParams(collective_id=0, has_side_effects=True),
    )(factor, right_sides, send_rows, neighbour_slot)
    written = jax.ShapeDtypeStruct((rows_here, columns), kept)
    return pl.pallas_call(
        write_out,
        out_shape=(written, written),
        in_specs=[pl.BlockSpec(memory_space=pltpu.VMEM)] * 2,
        out_specs=(pl.BlockSpec(memory_space=pl.ANY),) * 2,
        scratch_shapes=[pltpu.SemaphoreType.DMA((2,))],
        compiler_params=pltpu.CompilerParams(vmem_limit_bytes=1 << 20),
    )(half, full)


def move_rows(packed):
    moved = lax.all_to_all(
        lax.all_to_all(packed, "gy", split_axis=1, concat_axis=1, tiled=True),
        "gx",
        split_axis=0,
        concat_axis=0,
        tiled=True,
    )
    return moved


def move_sums(packed):
    moved = lax.all_to_all(
        lax.all_to_all(packed, "gy", split_axis=1, concat_axis=1, tiled=True),
        "gx",
        split_axis=0,
        concat_axis=0,
        tiled=True,
    )
    return moved


def shards(factor, right_sides, send_rows, neighbour_slot):
    blocks = factor.shape[0]
    width = factor.shape[1]
    far_width = factor.shape[2] - width
    senders = send_rows.shape[1]
    capacity = send_rows.shape[2]
    columns = right_sides.shape[1]
    outer = lax.axis_size("gx")
    inner = lax.axis_size("gy")
    places_all = senders * capacity
    rows_here = blocks * width
    tile = 256
    tiled = capacity % 16 == 0 and (inner * capacity) % 128 == 0 and places_all % tile == 0
    if tiled and width % tile == 0 and far_width % 128 == 0 and columns % 128 == 0:
        return fused(factor, right_sides, send_rows, neighbour_slot, tile)
    outgoing = send_rows.reshape(places_all)
    own_factor = factor[:, :, :width]
    far_factor = factor[:, :, width:]
    place_ids = jnp.arange(places_all, dtype=jnp.int32)
    picker = (neighbour_slot[:, :, None] == place_ids[None, None, :]).astype(jnp.bfloat16)
    spread_factor = jnp.einsum(
        "bij,bjs->bis", far_factor, picker, preferred_element_type=jnp.float32
    ).astype(jnp.bfloat16)
    row_ids = jnp.arange(rows_here, dtype=jnp.int32)
    selector = (outgoing[:, None] == row_ids[None, :]).astype(jnp.bfloat16)
    vector = right_sides
    own_rows = vector.reshape(blocks, width, columns)
    packed = jnp.dot(selector, vector, preferred_element_type=jnp.float32).astype(jnp.bfloat16)
    packed = packed.reshape(outer, inner, capacity, columns)
    received = move_rows(packed).reshape(places_all, columns)
    forward = jnp.einsum("bij,bjr->bir", own_factor, own_rows, preferred_element_type=jnp.float32)
    forward = forward + jnp.einsum(
        "bis,sr->bir", spread_factor, received, preferred_element_type=jnp.float32
    )
    weighted = forward.astype(jnp.bfloat16)
    own_back = jnp.einsum("bij,bir->bjr", own_factor, weighted, preferred_element_type=jnp.float32)
    slot_sums = jnp.einsum(
        "bis,bir->sr", spread_factor, weighted, preferred_element_type=jnp.float32
    )
    slot_sums = slot_sums.astype(jnp.bfloat16).reshape(outer, inner, capacity, columns)
    returned = move_sums(slot_sums).reshape(places_all, columns)
    added = jnp.einsum("sk,sr->kr", selector, returned, preferred_element_type=jnp.float32)
    vector = (own_back.reshape(rows_here, columns) + added).astype(jnp.bfloat16)
    return (weighted.reshape(rows_here, columns), vector)


def solution(mesh):
    in_specs = (
        P(("gx", "gy"), None, None),
        P(("gx", "gy"), None),
        P(("gx", "gy"), None, None),
        P(("gx", "gy"), None),
    )
    out_specs = (P(("gx", "gy"), None), P(("gx", "gy"), None))
    return jax.shard_map(shards, mesh=mesh, in_specs=in_specs, out_specs=out_specs, check_vma=False)
```

profile of v0, /device:TPU:0, one launch (start us, length us, event | category | flops | bytes accessed | tf_op | source)
XLA Modules:
  0.0 34.6 jit_solution(16155239490181247545)
XLA Ops:
  0.6 32.9 %shard_map.59 = (bf16[2048,128]{1,0:T(8,128)(2,1)S(1)}, bf16[2048,128]{1,0:T(8,128)(2,1)S(1)}) custom-call(bf16[8,256,768]{2,1,0:T(8,128)(2,1)} %factor_ref.1, bf16[2048,128]{1,0:T(8,128)(2,1)} %vector_ref.1, s32[1,32,48]{2,1,0:T(8,128)} %table_ref.1, s32[8,512]{1,0:T(8,128)} %slots_ref.1), custom_call_target="tpu_custom_call" | custom-call | tf_op jit(solution)/shard_map/pallas_call | solution.py:229
  33.6 1.0 %shard_map.60 = (bf16[2048,128]{1,0:T(8,128)(2,1)}, bf16[2048,128]{1,0:T(8,128)(2,1)}) custom-call(bf16[2048,128]{1,0:T(8,128)(2,1)S(1)} %get-tuple-element.4.half_ref, bf16[2048,128]{1,0:T(8,128)(2,1)S(1)} %get-tuple-element.5.full_ref), custom_call_target="tpu_custom_call" | custom-call | tf_op jit(solution)/shard_map/pallas_call | solution.py:250
where the time goes:
time: 34.9 us; the launch traced here: 34.6 us
  Pallas kernels  33.9 us (97%)
  between operations  0.64 us (2%)
    pallas_call x1, Pallas kernels, fused(): pl.pallas_call(functools.partial(kernel, outer, inner, tile), out_shape=(...  32.9 us
    pallas_call x1, Pallas kernels, fused(): pl.pallas_call(write_out, out_shape=(written, written), in_specs=[pl.Bloc...  0.99 us

commit v1 on v0

v1 whole, which is shorter than its diff:
```python
import functools

import jax
import jax.numpy as jnp
from jax import lax
from jax.experimental import pallas as pl
from jax.experimental.pallas import tpu as pltpu
from jax.sharding import PartitionSpec as P

MESH = pl.DeviceIdType.MESH
NT = (((1,), (1,)), ((), ()))
TN = (((0,), (0,)), ((), ()))


def one_hot(mask):
    return jnp.where(mask, 1.0, 0.0).astype(jnp.bfloat16)


def orders(outer):
    split = outer // 2

    def crosses(a, b):
        return (a < split) != (b < split)

    middle = (outer - 1) / 2
    rows, sums, waits = [], [], []
    for a in range(outer):
        every = range(outer)
        rows.append(sorted(every, key=lambda b: (abs(b - middle), not crosses(a, b), b)))
        sums.append(sorted(every, key=lambda b: (b != 0, not crosses(a, b), b == a, b)))
        waits.append(sorted((b for b in every if b != a), key=lambda b: (abs(b - a), b)))
    return rows, sums, waits


def kernel(
    outer, inner, tile,
    factor_ref, vector_ref, table_ref, slots_ref, half, full,
    factor, vector, table, slots, spread, spread_t, picker, packed, received, sums, returned,
    id_rows, id_columns, slot_columns, total, wide,
    load_sem, go_sem, back_go_sem, come_sem, back_come_sem,
):
    blocks, width, _ = factor.shape
    pairs, _ = vector.shape
    columns = half.shape[1]
    senders, capacity, _ = packed.shape
    places = senders * capacity
    span = inner * capacity
    far_width = slots.shape[1]
    side_blocks = blocks // 2
    gx, gy = lax.axis_index("gx"), lax.axis_index("gy")
    me = gx * inner + gy
    row_order, sum_order, wait_order = orders(outer)

    barrier = pltpu.get_barrier_semaphore()

    def greet(k, carry):
        other = lax.rem(me + k, senders)
        pl.semaphore_signal(
            barrier, inc=1, device_id=(other // inner, lax.rem(other, inner)), device_id_type=MESH
        )
        return carry

    loads = [
        pltpu.make_async_copy(table_ref, table, load_sem.at[0]),
        pltpu.make_async_copy(
            vector_ref.at[pl.ds(0, pairs)], vector.at[:, pl.ds(0, columns)], load_sem.at[1]
        ),
        pltpu.make_async_copy(
            vector_ref.at[pl.ds(pairs, pairs)], vector.at[:, pl.ds(columns, columns)], load_sem.at[2]
        ),
        pltpu.make_async_copy(slots_ref, slots, load_sem.at[3]),
        pltpu.make_async_copy(factor_ref, factor, load_sem.at[4]),
    ]
    for load in loads:
        load.start()
    lax.fori_loop(1, senders, greet, 0)

    received[me] = jnp.zeros((capacity, columns), jnp.bfloat16)
    returned[me] = jnp.zeros((capacity, columns), jnp.bfloat16)

    def listed(lists, k):
        plane = jnp.int32(lists[outer - 1][k])
        for i in range(outer - 1):
            plane = jnp.where(gx == i, jnp.int32(lists[i][k]), plane)
        return plane

    def group_places(g):
        return pl.ds(pl.multiple_of(g * span, 128), span)

    def group(ref, g):
        return ref[pl.ds(g * inner, inner)].reshape(span, columns)

    def send_group(source, target, send_sem, recv_sem, plane):
        def step(y, carry):
            to_y = lax.rem(gy + y, inner)
            pltpu.make_async_remote_copy(
                src_ref=source.at[plane * inner + to_y],
                dst_ref=target.at[me],
                send_sem=send_sem,
                recv_sem=recv_sem.at[gx],
                device_id=(plane, to_y),
                device_id_type=MESH,
            ).start()
            return carry

        lax.fori_loop(jnp.where(plane == gx, 1, 0), inner, step, 0)

    def await_bytes(buffer, sem, slabs):
        whole = buffer.at[pl.ds(0, slabs)]
        pltpu.make_async_copy(whole, whole, sem).wait()

    outward = (packed, received, go_sem, come_sem)
    inward = (sums, returned, back_go_sem, back_come_sem)

    loads[0].wait()
    flipped = table[0].T
    for e in range(senders):
        id_columns[pl.ds(e * capacity, capacity), :] = jnp.broadcast_to(
            flipped[:, e : e + 1], (capacity, 128)
        )
    loads[1].wait()
    loads[2].wait()

    def lanes(ids, n):
        return jnp.concatenate([ids] * (n // 128), axis=1)

    def pack(g):
        part = span // 2
        for r in range(2):
            ids = id_columns[pl.ds(pl.multiple_of(g * span + r * part, 8), part), :]
            upper = ids >= pairs
            ids = lanes(jnp.where(upper, ids - pairs, ids), tile)
            lane = lax.broadcasted_iota(jnp.int32, (part, tile), 1)
            rows = jnp.zeros((part, 2 * columns), jnp.float32)
            for c in range(pairs // tile):
                rows = rows + jnp.dot(
                    one_hot(ids == lane + c * tile),
                    vector[c * tile : (c + 1) * tile, :],
                    preferred_element_type=jnp.float32,
                )
            upper = lanes(upper.astype(jnp.int32), columns) > 0
            picked = jnp.where(upper, rows[:, columns:], rows[:, :columns])
            packed[pl.ds(g * inner + r * (inner // 2), inner // 2)] = picked.astype(
                jnp.bfloat16
            ).reshape(inner // 2, capacity, columns)

    for k in range(outer):
        plane = listed(row_order, k)
        pack(plane)
        if k == 0:
            pl.semaphore_wait(barrier, senders - 1)
        send_group(*outward, plane)

    loads[3].wait()
    slots_t = slots[...].T
    for b in range(blocks):
        slot_columns[b * far_width : (b + 1) * far_width, :] = jnp.broadcast_to(
            slots_t[:, b : b + 1], (far_width, 128)
        )
    loads[4].wait()

    def rows_of(side, b):
        return pl.ds(pl.multiple_of(b * width, width), width), slice(side * columns, (side + 1) * columns)

    def spread_block(side):
        def step(n, carry):
            b = side * side_blocks + n
            here = pl.ds(pl.multiple_of(b * width, width), width)
            far = factor[b, :, width:]
            ids = slots[pl.ds(b, 1), :]
            down = slot_columns[pl.ds(pl.multiple_of(b * far_width, 128), far_width), :]
            down = lanes(down, tile)
            lane = lax.broadcasted_iota(jnp.int32, (far_width, tile), 1)
            for c in range(places // tile):
                place = lax.broadcasted_iota(jnp.int32, (tile, far_width), 0) + c * tile
                there = slice(c * tile, (c + 1) * tile)
                spread_t[there, here] = lax.dot_general(
                    one_hot(ids == place), far, NT, preferred_element_type=jnp.float32
                ).astype(jnp.bfloat16)
                spread[here, there] = jnp.dot(
                    far, one_hot(down == lane + c * tile), preferred_element_type=jnp.float32
                ).astype(jnp.bfloat16)
            total[here, :] = jnp.dot(
                factor[b, :, :width], vector[rows_of(side, n)], preferred_element_type=jnp.float32
            )
            return carry

        lax.fori_loop(0, side_blocks, step, 0)

    for side in range(2):
        spread_block(side)

    id_rows[...] = jnp.concatenate([table[0, e : e + 1, :] for e in range(senders)], axis=1)
    id_rows[...] = jnp.where(id_rows[...] >= pairs, id_rows[...] - pairs, id_rows[...])

    def pick_rows(n, carry):
        here = pl.ds(pl.multiple_of(n * width, width), width)
        row = lax.broadcasted_iota(jnp.int32, (width, places), 0) + n * width
        picker[here, :] = one_hot(id_rows[0:1, :] == row)
        return carry

    lax.fori_loop(0, pairs // width, pick_rows, 0)

    slab = half.shape[0] // 2
    for n in range(outer):
        if n == 0:
            g = gx
            await_bytes(received, come_sem.at[g], inner - 1)
        else:
            g = listed(wait_order, n - 1)
            await_bytes(received, come_sem.at[g], inner)
        rows = group(received, g)
        for h in range(2):
            part = pl.ds(h * slab, slab)
            value = total[part, :] + jnp.dot(
                spread[part, group_places(g)], rows, preferred_element_type=jnp.float32
            )
            if n < outer - 1:
                total[part, :] = value
            else:
                half[part, :] = value.astype(jnp.bfloat16)

    for k in range(outer):
        g = listed(sum_order, k)
        value = jnp.dot(
            spread_t[pl.ds(pl.multiple_of(g * span, 128), span), :], half[...],
            preferred_element_type=jnp.float32,
        )
        sums[pl.ds(g * inner, inner)] = value.astype(jnp.bfloat16).reshape(inner, capacity, columns)
        send_group(*inward, g)

    def own_block(side):
        def step(n, carry):
            b = side * side_blocks + n
            here = pl.ds(pl.multiple_of(b * width, width), width)
            wide[rows_of(side, n)] = lax.dot_general(
                factor[b, :, :width], half[here, :], TN, preferred_element_type=jnp.float32
            )
            return carry

        lax.fori_loop(0, side_blocks, step, 0)

    for side in range(2):
        own_block(side)
    await_bytes(packed, go_sem, senders - 1)

    for n in range(outer):
        if n == 0:
            g = gx
            await_bytes(returned, back_come_sem.at[g], inner - 1)
        else:
            g = listed(wait_order, n - 1)
            await_bytes(returned, back_come_sem.at[g], inner)
        rows = group(returned, g)
        upper = lanes(id_columns[pl.ds(pl.multiple_of(g * span, 8), span), :], columns) >= pairs
        none = jnp.zeros_like(rows)
        both = jnp.concatenate([jnp.where(upper, none, rows), jnp.where(upper, rows, none)], axis=1)
        for h in range(2):
            part = pl.ds(h * (pairs // 2), pairs // 2)
            value = wide[part, :] + jnp.dot(
                picker[part, group_places(g)], both, preferred_element_type=jnp.float32
            )
            if n < outer - 1:
                wide[part, :] = value
            else:
                value = value.astype(jnp.bfloat16)
                full[part, :] = value[:, :columns]
                full[pl.ds(pairs + h * (pairs // 2), pairs // 2), :] = value[:, columns:]
    await_bytes(sums, back_go_sem, senders - 1)


def write_out(half_ref, full_ref, half_out, full_out, sems):
    copies = [
        pltpu.make_async_copy(half_ref, half_out, sems.at[0]),
        pltpu.make_async_copy(full_ref, full_out, sems.at[1]),
    ]
    for copy in copies:
        copy.start()
    for copy in copies:
        copy.wait()


def fused(factor, right_sides, send_rows, neighbour_slot, tile):
    blocks, width, _ = factor.shape
    rows_here, columns = right_sides.shape
    _, senders, capacity = send_rows.shape
    places = senders * capacity
    outer, inner = lax.axis_size("gx"), lax.axis_size("gy")
    kept = jnp.bfloat16
    out = pltpu.VMEM((rows_here, columns), kept)
    moved = pltpu.VMEM((senders, capacity, columns), kept)
    pairs, far_width = rows_here // 2, neighbour_slot.shape[1]
    flag, flags = pltpu.SemaphoreType.DMA, pltpu.SemaphoreType.DMA((outer,))
    half, full = pl.pallas_call(
        functools.partial(kernel, outer, inner, tile),
        out_shape=(out, out),
        in_specs=[pl.BlockSpec(memory_space=pl.ANY)] * 4,
        out_specs=(pl.BlockSpec(memory_space=pltpu.VMEM),) * 2,
        scratch_shapes=[
            pltpu.VMEM(factor.shape, kept),
            pltpu.VMEM((pairs, 2 * columns), kept),
            pltpu.VMEM(send_rows.shape, jnp.int32),
            pltpu.VMEM(neighbour_slot.shape, jnp.int32),
            pltpu.VMEM((rows_here, places), kept),
            pltpu.VMEM((places, rows_here), kept),
            pltpu.VMEM((pairs, places), kept),
            moved, moved, moved, moved,
            pltpu.VMEM((1, places), jnp.int32),
            pltpu.VMEM((places, 128), jnp.int32),
            pltpu.VMEM((blocks * far_width, 128), jnp.int32),
            pltpu.VMEM((rows_here, columns), jnp.float32),
            pltpu.VMEM((pairs, 2 * columns), jnp.float32),
            pltpu.SemaphoreType.DMA((5,)),
            flag, flag, flags, flags,
        ],
        compiler_params=pltpu.CompilerParams(collective_id=0, has_side_effects=True),
    )(factor, right_sides, send_rows, neighbour_slot)
    written = jax.ShapeDtypeStruct((rows_here, columns), kept)
    return pl.pallas_call(
        write_out,
        out_shape=(written, written),
        in_specs=[pl.BlockSpec(memory_space=pltpu.VMEM)] * 2,
        out_specs=(pl.BlockSpec(memory_space=pl.ANY),) * 2,
        scratch_shapes=[pltpu.SemaphoreType.DMA((2,))],
        compiler_params=pltpu.CompilerParams(vmem_limit_bytes=1 << 20),
    )(half, full)


def move_rows(packed):
    moved = lax.all_to_all(
        lax.all_to_all(packed, "gy", split_axis=1, concat_axis=1, tiled=True),
        "gx",
        split_axis=0,
        concat_axis=0,
        tiled=True,
    )
    return moved


def move_sums(packed):
    moved = lax.all_to_all(
        lax.all_to_all(packed, "gy", split_axis=1, concat_axis=1, tiled=True),
        "gx",
        split_axis=0,
        concat_axis=0,
        tiled=True,
    )
    return moved


def shards(factor, right_sides, send_rows, neighbour_slot):
    blocks = factor.shape[0]
    width = factor.shape[1]
    far_width = factor.shape[2] - width
    senders = send_rows.shape[1]
    capacity = send_rows.shape[2]
    columns = right_sides.shape[1]
    outer = lax.axis_size("gx")
    inner = lax.axis_size("gy")
    places_all = senders * capacity
    rows_here = blocks * width
    tile = 256
    tiled = capacity % 16 == 0 and (inner * capacity) % 128 == 0
    tiled = tiled and inner % 2 == 0 and blocks % 2 == 0 and places_all % tile == 0
    if tiled and width % tile == 0 and far_width % 128 == 0 and columns % 128 == 0:
        return fused(factor, right_sides, send_rows, neighbour_slot, tile)
    outgoing = send_rows.reshape(places_all)
    own_factor = factor[:, :, :width]
    far_factor = factor[:, :, width:]
    place_ids = jnp.arange(places_all, dtype=jnp.int32)
    picker = (neighbour_slot[:, :, None] == place_ids[None, None, :]).astype(jnp.bfloat16)
    spread_factor = jnp.einsum(
        "bij,bjs->bis", far_factor, picker, preferred_element_type=jnp.float32
    ).astype(jnp.bfloat16)
    row_ids = jnp.arange(rows_here, dtype=jnp.int32)
    selector = (outgoing[:, None] == row_ids[None, :]).astype(jnp.bfloat16)
    vector = right_sides
    own_rows = vector.reshape(blocks, width, columns)
    packed = jnp.dot(selector, vector, preferred_element_type=jnp.float32).astype(jnp.bfloat16)
    packed = packed.reshape(outer, inner, capacity, columns)
    received = move_rows(packed).reshape(places_all, columns)
    forward = jnp.einsum("bij,bjr->bir", own_factor, own_rows, preferred_element_type=jnp.float32)
    forward = forward + jnp.einsum(
        "bis,sr->bir", spread_factor, received, preferred_element_type=jnp.float32
    )
    weighted = forward.astype(jnp.bfloat16)
    own_back = jnp.einsum("bij,bir->bjr", own_factor, weighted, preferred_element_type=jnp.float32)
    slot_sums = jnp.einsum(
        "bis,bir->sr", spread_factor, weighted, preferred_element_type=jnp.float32
    )
    slot_sums = slot_sums.astype(jnp.bfloat16).reshape(outer, inner, capacity, columns)
    returned = move_sums(slot_sums).reshape(places_all, columns)
    added = jnp.einsum("sk,sr->kr", selector, returned, preferred_element_type=jnp.float32)
    vector = (own_back.reshape(rows_here, columns) + added).astype(jnp.bfloat16)
    return (weighted.reshape(rows_here, columns), vector)


def solution(mesh):
    in_specs = (
        P(("gx", "gy"), None, None),
        P(("gx", "gy"), None),
        P(("gx", "gy"), None, None),
        P(("gx", "gy"), None),
    )
    out_specs = (P(("gx", "gy"), None), P(("gx", "gy"), None))
    return jax.shard_map(shards, mesh=mesh, in_specs=in_specs, out_specs=out_specs, check_vma=False)
```

time: 34.9 us -> 32.9 us (0.943)
  the two profiles are of different devices: /device:TPU:0 before, /device:TPU:24 now
where the time goes in v1:
time: 32.9 us; the launch traced here: 32.4 us
  Pallas kernels  31.7 us (96%)
  between operations  0.64 us (2%)
    pallas_call x1, Pallas kernels, fused(): pl.pallas_call(functools.partial(kernel, outer, inner, tile), out_shape=(...  30.7 us
    pallas_call x1, Pallas kernels, fused(): pl.pallas_call(write_out, out_shape=(written, written), in_specs=[pl.Bloc...  0.99 us

profile of v1, /device:TPU:24, one launch (start us, length us, event | category | flops | bytes accessed | tf_op | source)
XLA Modules:
  0.0 32.4 jit_solution(17057461552572708842)
XLA Ops:
  0.6 30.7 %shard_map.59 = (bf16[2048,128]{1,0:T(8,128)(2,1)S(1)}, bf16[2048,128]{1,0:T(8,128)(2,1)S(1)}) custom-call(bf16[8,256,768]{2,1,0:T(8,128)(2,1)} %factor_ref.1, bf16[2048,128]{1,0:T(8,128)(2,1)} %vector_ref.1, s32[1,32,48]{2,1,0:T(8,128)} %table_ref.1, s32[8,512]{1,0:T(8,128)} %slots_ref.1), custom_call_target="tpu_custom_call" | custom-call | tf_op jit(solution)/shard_map/pallas_call | solution.py:294
  31.4 1.0 %shard_map.60 = (bf16[2048,128]{1,0:T(8,128)(2,1)}, bf16[2048,128]{1,0:T(8,128)(2,1)}) custom-call(bf16[2048,128]{1,0:T(8,128)(2,1)S(1)} %get-tuple-element.4.half_ref, bf16[2048,128]{1,0:T(8,128)(2,1)S(1)} %get-tuple-element.5.full_ref), custom_call_target="tpu_custom_call" | custom-call | tf_op jit(solution)/shard_map/pallas_call | solution.py:319

commit v2 on v1

--- a/solution.py
+++ b/solution.py
@@ -12,8 +12,23 @@
 TN = (((0,), (0,)), ((), ()))
 
 
-def one_hot(mask):
-    return jnp.where(mask, 1.0, 0.0).astype(jnp.bfloat16)
+def one_hot(ids, places):
+    one, zero = jnp.bfloat16(1), jnp.bfloat16(0)
+    return jnp.where(ids == places, one, zero)
+
+
+def whole(ids):
+    return ids.astype(jnp.float32).astype(jnp.bfloat16)
+
+
+def within(ids, first, size):
+    ids = ids - first
+    return whole(jnp.where((ids >= 0) & (ids < size), ids, -1))
+
+
+def count(n, axis):
+    shape = (n, 128) if axis == 0 else (16, n)
+    return whole(lax.broadcasted_iota(jnp.int32, shape, axis))
 
 
 def orders(outer):
@@ -27,7 +42,10 @@
     for a in range(outer):
         every = range(outer)
         rows.append(sorted(every, key=lambda b: (abs(b - middle), not crosses(a, b), b)))
-        sums.append(sorted(every, key=lambda b: (b != 0, not crosses(a, b), b == a, b)))
+        near = a == split
+        sums.append(
+            sorted(every, key=lambda b: (near and not crosses(a, b), near and b == a, abs(b - a) if near else b))
+        )
         waits.append(sorted((b for b in every if b != a), key=lambda b: (abs(b - a), b)))
     return rows, sums, waits
 
@@ -35,8 +53,8 @@
 def kernel(
     outer, inner, tile,
     factor_ref, vector_ref, table_ref, slots_ref, half, full,
-    factor, vector, table, slots, spread, spread_t, picker, packed, received, sums, returned,
-    id_rows, id_columns, slot_columns, total, wide,
+    factor, vector, table, slots, spread_t, picker, packed, received, sums, returned,
+    id_rows, id_columns, total_t, half_t, wide,
     load_sem, go_sem, back_go_sem, come_sem, back_come_sem,
 ):
     blocks, width, _ = factor.shape
@@ -124,17 +142,19 @@
     def lanes(ids, n):
         return jnp.concatenate([ids] * (n // 128), axis=1)
 
+    def lane_count(n):
+        return jnp.concatenate([count(tile, 1)] * (n // 16), axis=0)
+
     def pack(g):
         part = span // 2
         for r in range(2):
             ids = id_columns[pl.ds(pl.multiple_of(g * span + r * part, 8), part), :]
             upper = ids >= pairs
-            ids = lanes(jnp.where(upper, ids - pairs, ids), tile)
-            lane = lax.broadcasted_iota(jnp.int32, (part, tile), 1)
+            ids = jnp.where(upper, ids - pairs, ids)
             rows = jnp.zeros((part, 2 * columns), jnp.float32)
             for c in range(pairs // tile):
                 rows = rows + jnp.dot(
-                    one_hot(ids == lane + c * tile),
+                    one_hot(lanes(within(ids, c * tile, tile), tile), lane_count(part)),
                     vector[c * tile : (c + 1) * tile, :],
                     preferred_element_type=jnp.float32,
                 )
@@ -152,11 +172,6 @@
         send_group(*outward, plane)
 
     loads[3].wait()
-    slots_t = slots[...].T
-    for b in range(blocks):
-        slot_columns[b * far_width : (b + 1) * far_width, :] = jnp.broadcast_to(
-            slots_t[:, b : b + 1], (far_width, 128)
-        )
     loads[4].wait()
 
     def rows_of(side, b):
@@ -168,20 +183,20 @@
             here = pl.ds(pl.multiple_of(b * width, width), width)
             far = factor[b, :, width:]
             ids = slots[pl.ds(b, 1), :]
-            down = slot_columns[pl.ds(pl.multiple_of(b * far_width, 128), far_width), :]
-            down = lanes(down, tile)
-            lane = lax.broadcasted_iota(jnp.int32, (far_width, tile), 1)
-            for c in range(places // tile):
-                place = lax.broadcasted_iota(jnp.int32, (tile, far_width), 0) + c * tile
-                there = slice(c * tile, (c + 1) * tile)
-                spread_t[there, here] = lax.dot_general(
-                    one_hot(ids == place), far, NT, preferred_element_type=jnp.float32
+            for c in range(0, places, 1536):
+                hot = [
+                    one_hot(
+                        jnp.broadcast_to(within(ids, d, tile), (tile, far_width)),
+                        lanes(count(tile, 0), far_width),
+                    )
+                    for d in range(c, c + 1536, tile)
+                ]
+                spread_t[c : c + 1536, here] = lax.dot_general(
+                    jnp.concatenate(hot, axis=0), far, NT, preferred_element_type=jnp.float32
                 ).astype(jnp.bfloat16)
-                spread[here, there] = jnp.dot(
-                    far, one_hot(down == lane + c * tile), preferred_element_type=jnp.float32
-                ).astype(jnp.bfloat16)
-            total[here, :] = jnp.dot(
-                factor[b, :, :width], vector[rows_of(side, n)], preferred_element_type=jnp.float32
+            total_t[:, here] = lax.dot_general(
+                vector[rows_of(side, n)], factor[b, :, :width], (((0,), (1,)), ((), ())),
+                preferred_element_type=jnp.float32,
             )
             return carry
 
@@ -190,18 +205,7 @@
     for side in range(2):
         spread_block(side)
 
-    id_rows[...] = jnp.concatenate([table[0, e : e + 1, :] for e in range(senders)], axis=1)
-    id_rows[...] = jnp.where(id_rows[...] >= pairs, id_rows[...] - pairs, id_rows[...])
-
-    def pick_rows(n, carry):
-        here = pl.ds(pl.multiple_of(n * width, width), width)
-        row = lax.broadcasted_iota(jnp.int32, (width, places), 0) + n * width
-        picker[here, :] = one_hot(id_rows[0:1, :] == row)
-        return carry
-
-    lax.fori_loop(0, pairs // width, pick_rows, 0)
-
-    slab = half.shape[0] // 2
+    slab = half.shape[0] // 4
     for n in range(outer):
         if n == 0:
             g = gx
@@ -209,22 +213,21 @@
         else:
             g = listed(wait_order, n - 1)
             await_bytes(received, come_sem.at[g], inner)
-        rows = group(received, g)
-        for h in range(2):
-            part = pl.ds(h * slab, slab)
-            value = total[part, :] + jnp.dot(
-                spread[part, group_places(g)], rows, preferred_element_type=jnp.float32
+        rows_t = group(received, g).T
+        for h in range(4):
+            part = slice(h * slab, (h + 1) * slab)
+            value = total_t[:, part] + jnp.dot(
+                rows_t, spread_t[group_places(g), part], preferred_element_type=jnp.float32
             )
             if n < outer - 1:
-                total[part, :] = value
+                total_t[:, part] = value
             else:
-                half[part, :] = value.astype(jnp.bfloat16)
+                half_t[:, part] = value.astype(jnp.bfloat16)
 
     for k in range(outer):
         g = listed(sum_order, k)
-        value = jnp.dot(
-            spread_t[pl.ds(pl.multiple_of(g * span, 128), span), :], half[...],
-            preferred_element_type=jnp.float32,
+        value = lax.dot_general(
+            spread_t[group_places(g), :], half_t[...], NT, preferred_element_type=jnp.float32
         )
         sums[pl.ds(g * inner, inner)] = value.astype(jnp.bfloat16).reshape(inner, capacity, columns)
         send_group(*inward, g)
@@ -240,8 +243,20 @@
 
         lax.fori_loop(0, side_blocks, step, 0)
 
+    half[...] = half_t[...].T
     for side in range(2):
         own_block(side)
+    id_rows[...] = jnp.concatenate([table[0, e : e + 1, :] for e in range(senders)], axis=1)
+    id_rows[...] = jnp.where(id_rows[...] >= pairs, id_rows[...] - pairs, id_rows[...])
+
+    def pick_rows(n, carry):
+        here = pl.ds(pl.multiple_of(n * width, width), width)
+        ids = jnp.broadcast_to(within(id_rows[0:1, :], n * width, width), (width, places))
+        picker[here, :] = one_hot(ids, lanes(count(width, 0), places))
+        return carry
+
+    lax.fori_loop(0, pairs // width, pick_rows, 0)
+
     await_bytes(packed, go_sem, senders - 1)
 
     for n in range(outer):
@@ -301,14 +316,13 @@
             pltpu.VMEM((pairs, 2 * columns), kept),
             pltpu.VMEM(send_rows.shape, jnp.int32),
             pltpu.VMEM(neighbour_slot.shape, jnp.int32),
-            pltpu.VMEM((rows_here, places), kept),
             pltpu.VMEM((places, rows_here), kept),
             pltpu.VMEM((pairs, places), kept),
             moved, moved, moved, moved,
             pltpu.VMEM((1, places), jnp.int32),
             pltpu.VMEM((places, 128), jnp.int32),
-            pltpu.VMEM((blocks * far_width, 128), jnp.int32),
-            pltpu.VMEM((rows_here, columns), jnp.float32),
+            pltpu.VMEM((columns, rows_here), jnp.float32),
+            pltpu.VMEM((columns, rows_here), kept),
             pltpu.VMEM((pairs, 2 * columns), jnp.float32),
             pltpu.SemaphoreType.DMA((5,)),
             flag, flag, flags, flags,

time: 32.9 us -> 29.7 us (0.903)
  Pallas kernels: 31.7 us -> 28.5 us
    pallas_call x1, Pallas kernels: 30.7 us -> 27.6 us  [fused(): pl.pallas_call(functools.partial(kernel, outer, inner, tile), out_shape=(...]
where the time goes in v2:
time: 29.7 us; the launch traced here: 29.2 us
  Pallas kernels  28.5 us (96%)
  between operations  0.64 us (2%)
    pallas_call x1, Pallas kernels, fused(): pl.pallas_call(functools.partial(kernel, outer, inner, tile), out_shape=(...  27.6 us
    pallas_call x1, Pallas kernels, fused(): pl.pallas_call(write_out, out_shape=(written, written), in_specs=[pl.Bloc...  0.99 us

profile of v2, /device:TPU:24, one launch (start us, length us, event | category | flops | bytes accessed | tf_op | source)
XLA Modules:
  0.0 29.2 jit_solution(601476783492188282)
XLA Ops:
  0.6 27.6 %shard_map.59 = (bf16[2048,128]{1,0:T(8,128)(2,1)S(1)}, bf16[2048,128]{1,0:T(8,128)(2,1)S(1)}) custom-call(bf16[8,256,768]{2,1,0:T(8,128)(2,1)} %factor_ref.1, bf16[2048,128]{1,0:T(8,128)(2,1)} %vector_ref.1, s32[1,32,48]{2,1,0:T(8,128)} %table_ref.1, s32[8,512]{1,0:T(8,128)} %slots_ref.1), custom_call_target="tpu_custom_call" | custom-call | tf_op jit(solution)/shard_map/pallas_call | solution.py:309
  28.2 1.0 %shard_map.60 = (bf16[2048,128]{1,0:T(8,128)(2,1)}, bf16[2048,128]{1,0:T(8,128)(2,1)}) custom-call(bf16[2048,128]{1,0:T(8,128)(2,1)S(1)} %get-tuple-element.4.half_ref, bf16[2048,128]{1,0:T(8,128)(2,1)S(1)} %get-tuple-element.5.full_ref), custom_call_target="tpu_custom_call" | custom-call | tf_op jit(solution)/shard_map/pallas_call | solution.py:333

commit v3 on v2

--- a/solution.py
+++ b/solution.py
@@ -37,15 +37,18 @@
     def crosses(a, b):
         return (a < split) != (b < split)
 
-    middle = (outer - 1) / 2
+    middle, last = (outer - 1) / 2, outer - 1
     rows, sums, waits = [], [], []
     for a in range(outer):
         every = range(outer)
-        rows.append(sorted(every, key=lambda b: (abs(b - middle), not crosses(a, b), b)))
-        near = a == split
-        sums.append(
-            sorted(every, key=lambda b: (near and not crosses(a, b), near and b == a, abs(b - a) if near else b))
-        )
+        aside = split <= a < last
+        rows.append(
+            sorted(
+                every,
+                key=lambda b: (b == last, aside or abs(b - middle), not crosses(a, b), abs(b - a) if aside else b),
+            )
+        )
+        sums.append(sorted(every, key=lambda b: (b >= split, b if b < split or a == split - 1 else -b)))
         waits.append(sorted((b for b in every if b != a), key=lambda b: (abs(b - a), b)))
     return rows, sums, waits
 
@@ -55,7 +58,7 @@
     factor_ref, vector_ref, table_ref, slots_ref, half, full,
     factor, vector, table, slots, spread_t, picker, packed, received, sums, returned,
     id_rows, id_columns, total_t, half_t, wide,
-    load_sem, go_sem, back_go_sem, come_sem, back_come_sem,
+    load_sem, late_sem, go_sem, back_go_sem, come_sem, back_come_sem,
 ):
     blocks, width, _ = factor.shape
     pairs, _ = vector.shape
@@ -91,7 +94,34 @@
     ]
     for load in loads:
         load.start()
-    lax.fori_loop(1, senders, greet, 0)
+    last = outer - 1
+    early = last * inner
+    is_last = gx == last
+    lax.fori_loop(1, jnp.where(is_last, 1, senders), greet, 0)
+
+    def greet_plane(y, carry):
+        pl.semaphore_signal(
+            barrier, inc=1, device_id=(gx, lax.rem(gy + y, inner)), device_id_type=MESH
+        )
+        return carry
+
+    lax.fori_loop(1, jnp.where(is_last, inner, 1), greet_plane, 0)
+
+    def announce(k, carry):
+        pl.semaphore_signal(
+            late_sem, inc=1, device_id=(k // inner, lax.rem(k, inner)), device_id_type=MESH
+        )
+        return carry
+
+    def meet():
+        @pl.when(is_last)
+        def _():
+            pl.semaphore_wait(barrier, senders - 1)
+            lax.fori_loop(0, early, announce, 0)
+
+        @pl.when(jnp.logical_not(is_last))
+        def _():
+            pl.semaphore_wait(barrier, early - 1)
 
     received[me] = jnp.zeros((capacity, columns), jnp.bfloat16)
     returned[me] = jnp.zeros((capacity, columns), jnp.bfloat16)
@@ -109,7 +139,7 @@
         return ref[pl.ds(g * inner, inner)].reshape(span, columns)
 
     def send_group(source, target, send_sem, recv_sem, plane):
-        def step(y, carry):
+        def send(y):
             to_y = lax.rem(gy + y, inner)
             pltpu.make_async_remote_copy(
                 src_ref=source.at[plane * inner + to_y],
@@ -119,9 +149,13 @@
                 device_id=(plane, to_y),
                 device_id_type=MESH,
             ).start()
-            return carry
-
-        lax.fori_loop(jnp.where(plane == gx, 1, 0), inner, step, 0)
+
+        for y in range(1, inner):
+            send(y)
+
+        @pl.when(plane != gx)
+        def _():
+            send(0)
 
     def await_bytes(buffer, sem, slabs):
         whole = buffer.at[pl.ds(0, slabs)]
@@ -168,7 +202,12 @@
         plane = listed(row_order, k)
         pack(plane)
         if k == 0:
-            pl.semaphore_wait(barrier, senders - 1)
+            meet()
+
+        @pl.when((plane == last) & jnp.logical_not(is_last))
+        def _():
+            pl.semaphore_wait(late_sem, inner)
+
         send_group(*outward, plane)
 
     loads[3].wait()
@@ -325,6 +364,7 @@
             pltpu.VMEM((columns, rows_here), kept),
             pltpu.VMEM((pairs, 2 * columns), jnp.float32),
             pltpu.SemaphoreType.DMA((5,)),
+            pltpu.SemaphoreType.REGULAR,
             flag, flag, flags, flags,
         ],
         compiler_params=pltpu.CompilerParams(collective_id=0, has_side_effects=True),
@@ -375,7 +415,7 @@
     rows_here = blocks * width
     tile = 256
     tiled = capacity % 16 == 0 and (inner * capacity) % 128 == 0
-    tiled = tiled and inner % 2 == 0 and blocks % 2 == 0 and places_all % tile == 0
+    tiled = tiled and outer > 1 and inner % 2 == 0 and blocks % 2 == 0 and places_all % tile == 0
     if tiled and width % tile == 0 and far_width % 128 == 0 and columns % 128 == 0:
         return fused(factor, right_sides, send_rows, neighbour_slot, tile)
     outgoing = send_rows.reshape(places_all)

time: 29.7 us -> 28.5 us (0.960)
  the two profiles are of different devices: /device:TPU:24 before, /device:TPU:17 now
where the time goes in v3:
time: 28.5 us; the launch traced here: 28.3 us
  Pallas kernels  27.6 us (97%)
  between operations  0.64 us (2%)
    pallas_call x1, Pallas kernels, fused(): pl.pallas_call(functools.partial(kernel, outer, inner, tile), out_shape=(...  26.6 us
    pallas_call x1, Pallas kernels, fused(): pl.pallas_call(write_out, out_shape=(written, written), in_specs=[pl.Bloc...  0.99 us

profile of v3, /device:TPU:17, one launch (start us, length us, event | category | flops | bytes accessed | tf_op | source)
XLA Modules:
  0.0 28.3 jit_solution(7351542953182072115)
XLA Ops:
  0.6 26.6 %shard_map.59 = (bf16[2048,128]{1,0:T(8,128)(2,1)S(1)}, bf16[2048,128]{1,0:T(8,128)(2,1)S(1)}) custom-call(bf16[8,256,768]{2,1,0:T(8,128)(2,1)} %factor_ref.1, bf16[2048,128]{1,0:T(8,128)(2,1)} %vector_ref.1, s32[1,32,48]{2,1,0:T(8,128)} %table_ref.1, s32[8,512]{1,0:T(8,128)} %slots_ref.1), custom_call_target="tpu_custom_call" | custom-call | tf_op jit(solution)/shard_map/pallas_call | solution.py:348
  27.3 1.0 %shard_map.60 = (bf16[2048,128]{1,0:T(8,128)(2,1)}, bf16[2048,128]{1,0:T(8,128)(2,1)}) custom-call(bf16[2048,128]{1,0:T(8,128)(2,1)S(1)} %get-tuple-element.4.half_ref, bf16[2048,128]{1,0:T(8,128)(2,1)S(1)} %get-tuple-element.5.full_ref), custom_call_target="tpu_custom_call" | custom-call | tf_op jit(solution)/shard_map/pallas_call | solution.py:373

commit v4 on v3

--- a/solution.py
+++ b/solution.py
@@ -48,7 +48,7 @@
                 key=lambda b: (b == last, aside or abs(b - middle), not crosses(a, b), abs(b - a) if aside else b),
             )
         )
-        sums.append(sorted(every, key=lambda b: (b >= split, b if b < split or a == split - 1 else -b)))
+        sums.append(sorted(every, key=lambda b: (b >= split, b if b < split or a in (split - 1, last) else -b)))
         waits.append(sorted((b for b in every if b != a), key=lambda b: (abs(b - a), b)))
     return rows, sums, waits
 
@@ -140,7 +140,7 @@
 
     def send_group(source, target, send_sem, recv_sem, plane):
         def send(y):
-            to_y = lax.rem(gy + y, inner)
+            to_y = lax.rem(gy + inner - y, inner)
             pltpu.make_async_remote_copy(
                 src_ref=source.at[plane * inner + to_y],
                 dst_ref=target.at[me],

time: 28.5 us -> 28.1 us (0.986)
  the two profiles are of different devices: /device:TPU:17 before, /device:TPU:24 now
where the time goes in v4:
time: 28.1 us; the launch traced here: 27.9 us
  Pallas kernels  27.3 us (97%)
  between operations  0.64 us (2%)
    pallas_call x1, Pallas kernels, fused(): pl.pallas_call(functools.partial(kernel, outer, inner, tile), out_shape=(...  26.3 us
    pallas_call x1, Pallas kernels, fused(): pl.pallas_call(write_out, out_shape=(written, written), in_specs=[pl.Bloc...  0.99 us

profile of v4, /device:TPU:24, one launch (start us, length us, event | category | flops | bytes accessed | tf_op | source)
XLA Modules:
  0.0 27.9 jit_solution(11105402587617994411)
XLA Ops:
  0.6 26.3 %shard_map.59 = (bf16[2048,128]{1,0:T(8,128)(2,1)S(1)}, bf16[2048,128]{1,0:T(8,128)(2,1)S(1)}) custom-call(bf16[8,256,768]{2,1,0:T(8,128)(2,1)} %factor_ref.1, bf16[2048,128]{1,0:T(8,128)(2,1)} %vector_ref.1, s32[1,32,48]{2,1,0:T(8,128)} %table_ref.1, s32[8,512]{1,0:T(8,128)} %slots_ref.1), custom_call_target="tpu_custom_call" | custom-call | tf_op jit(solution)/shard_map/pallas_call | solution.py:348
  26.9 1.0 %shard_map.60 = (bf16[2048,128]{1,0:T(8,128)(2,1)}, bf16[2048,128]{1,0:T(8,128)(2,1)}) custom-call(bf16[2048,128]{1,0:T(8,128)(2,1)S(1)} %get-tuple-element.4.half_ref, bf16[2048,128]{1,0:T(8,128)(2,1)S(1)} %get-tuple-element.5.full_ref), custom_call_target="tpu_custom_call" | custom-call | tf_op jit(solution)/shard_map/pallas_call | solution.py:373

commit v5 on v4

--- a/solution.py
+++ b/solution.py
@@ -244,7 +244,7 @@
     for side in range(2):
         spread_block(side)
 
-    slab = half.shape[0] // 4
+    slab = half.shape[0] // 2
     for n in range(outer):
         if n == 0:
             g = gx
@@ -253,7 +253,7 @@
             g = listed(wait_order, n - 1)
             await_bytes(received, come_sem.at[g], inner)
         rows_t = group(received, g).T
-        for h in range(4):
+        for h in range(2):
             part = slice(h * slab, (h + 1) * slab)
             value = total_t[:, part] + jnp.dot(
                 rows_t, spread_t[group_places(g), part], preferred_element_type=jnp.float32
@@ -324,9 +324,14 @@
 
 
 def write_out(half_ref, full_ref, half_out, full_out, sems):
+    pieces = sems.shape[0] // 2
+    size = half_ref.shape[0] // pieces
     copies = [
-        pltpu.make_async_copy(half_ref, half_out, sems.at[0]),
-        pltpu.make_async_copy(full_ref, full_out, sems.at[1]),
+        pltpu.make_async_copy(
+            source.at[pl.ds(n * size, size)], target.at[pl.ds(n * size, size)], sems.at[n + first]
+        )
+        for source, target, first in ((half_ref, half_out, 0), (full_ref, full_out, pieces))
+        for n in range(pieces)
     ]
     for copy in copies:
         copy.start()
@@ -375,7 +380,7 @@
         out_shape=(written, written),
         in_specs=[pl.BlockSpec(memory_space=pltpu.VMEM)] * 2,
         out_specs=(pl.BlockSpec(memory_space=pl.ANY),) * 2,
-        scratch_shapes=[pltpu.SemaphoreType.DMA((2,))],
+        scratch_shapes=[pltpu.SemaphoreType.DMA((8,))],
         compiler_params=pltpu.CompilerParams(vmem_limit_bytes=1 << 20),
     )(half, full)
 

time: 28.1 us -> 28.2 us (level)
  no operation moved by 1% of the time
where the time goes in v5:
time: 28.2 us; the launch traced here: 27.9 us
  Pallas kernels  27.3 us (97%)
  between operations  0.64 us (2%)
    pallas_call x1, Pallas kernels, fused(): pl.pallas_call(functools.partial(kernel, outer, inner, tile), out_shape=(...  26.3 us
    pallas_call x1, Pallas kernels, fused(): pl.pallas_call(write_out, out_shape=(written, written), in_specs=[pl.Bloc...  1.03 us

profile of v5, /device:TPU:24, one launch (start us, length us, event | category | flops | bytes accessed | tf_op | source)
XLA Modules:
  0.0 27.9 jit_solution(10274343042048630782)
XLA Ops:
  0.6 26.3 %shard_map.59 = (bf16[2048,128]{1,0:T(8,128)(2,1)S(1)}, bf16[2048,128]{1,0:T(8,128)(2,1)S(1)}) custom-call(bf16[8,256,768]{2,1,0:T(8,128)(2,1)} %factor_ref.1, bf16[2048,128]{1,0:T(8,128)(2,1)} %vector_ref.1, s32[1,32,48]{2,1,0:T(8,128)} %table_ref.1, s32[8,512]{1,0:T(8,128)} %slots_ref.1), custom_call_target="tpu_custom_call" | custom-call | tf_op jit(solution)/shard_map/pallas_call | solution.py:353
  26.9 1.0 %shard_map.60 = (bf16[2048,128]{1,0:T(8,128)(2,1)}, bf16[2048,128]{1,0:T(8,128)(2,1)}) custom-call(bf16[2048,128]{1,0:T(8,128)(2,1)S(1)} %get-tuple-element.4.half_ref, bf16[2048,128]{1,0:T(8,128)(2,1)S(1)} %get-tuple-element.5.full_ref), custom_call_target="tpu_custom_call" | custom-call | tf_op jit(solution)/shard_map/pallas_call | solution.py:378
